TPU v7x, 32 devices: a whole 2x2x4 slice. The times are simulated.
32 devices in a mesh: groups: 2 (over y), seq: 4 (over z), head: 2 (over x), layer: 2 (over core).
Axes of the slice: x: 2, y: 2, z: 4, core: 2. Of those that a mesh axis runs over, the one named last changes fastest.
Arguments:
- kv_cache: bfloat16 [2, 2, 8, 4096, 2, 128], P(None, 'layer', 'groups', 'seq', 'head'), parts along dimension 2, may hold values from -800 to 800
- valid_blocks: int32 [8], P('groups'), parts along dimension 0, may hold values from 1 to 32, 64 in all
Outputs:
- decode_cache: bfloat16 [2, 2, 8, 4096, 2, 128], P(None, 'layer', ('groups', 'seq'), None, 'head'), parts along dimension 2
- centers: float32 [2, 2, 8, 2, 128], P(None, 'layer', 'groups', 'head'), parts along dimension 2
- scales: float32 [2, 2, 8, 2, 128], P(None, 'layer', 'groups', 'head'), parts along dimension 2
There are 2 independent parts, one for each index of `groups`. A program takes and returns all parts, laid end to end along the dimension named above; each array names one. Nothing has to cross between parts.
Inputs may be any that keep to these rules, and one draw needn't show every extreme that they name: `valid_blocks`: the counts of the 4 users sum to 64, and the largest equals 32.
All inputs are finite; a program needn't handle non-finite values.
Results may differ from a plain program's by a relative error of at most 0.001.
Values may be sent and summed in bfloat16 or wider, within the bound.
A program may use at most 64 MiB of HBM per device.

v0:
```python
import functools

import jax
import jax.numpy as jnp
from jax import lax
from jax.experimental import pallas as pl
from jax.experimental.pallas import tpu as pltpu
from jax.sharding import PartitionSpec as P

BLOCK = 128
ROWS = 8
CHUNK = 256
GRANT = 16 * 2**20
EPSILON = 1e-06


def normalised(recv_ref, k, rows, first, length, center, inverse):
    x = recv_ref[k, rows, :].astype(jnp.float32)
    position = first + lax.broadcasted_iota(jnp.int32, x.shape, 0)
    return jnp.where(position < length, (x - center) * inverse, 0.0).astype(jnp.bfloat16)


def last_source(me, n):
    return jnp.where(me < n - 1 - me, n - 1, 0)


def transport(n, quarter, chunk, blocks_ref, kv_ref, recv_ref, centers_ref, scales_ref,
              inverse_ref, length_ref, stats_ref, blocks, local, load_sem, blocks_sem, own_sem, send_sem, recv_sem,
              stat_send, stat_recv):
    kinds, users, per_dev, width = kv_ref.shape
    part = per_dev // quarter
    me = lax.axis_index("seq")

    load = pltpu.make_async_copy(kv_ref, local, load_sem)
    load.start()
    fetch = pltpu.make_async_copy(blocks_ref, blocks, blocks_sem)
    fetch.start()

    barrier = pltpu.get_barrier_semaphore()
    for d in range(n):
        @pl.when(me != d)
        def _():
            pl.semaphore_signal(barrier, inc=1, device_id={"seq": d})
    pl.semaphore_wait(barrier, n - 1)

    def bulk(source, target, k):
        user, q = target // quarter, target % quarter
        return pltpu.make_async_remote_copy(
            src_ref=kv_ref.at[k, user, pl.ds(pl.multiple_of(q * part, part), part), :],
            dst_ref=recv_ref.at[k, pl.ds(pl.multiple_of(source * part, part), part), :],
            send_sem=send_sem.at[target, k],
            recv_sem=recv_sem.at[source, k],
            device_id={"seq": target},
        )

    def stat(source, target):
        return pltpu.make_async_remote_copy(
            src_ref=stats_ref.at[source],
            dst_ref=stats_ref.at[source],
            send_sem=stat_send.at[target],
            recv_sem=stat_recv.at[source],
            device_id={"seq": target},
        )

    def start_bulk(dist):
        for k in range(kinds):
            @pl.when(me + dist < n)
            def _():
                bulk(me, me + dist, k).start()

            @pl.when(me - dist >= 0)
            def _():
                bulk(me, me - dist, k).start()

    start_bulk(1)
    own = pltpu.make_async_copy(
        kv_ref.at[:, me // quarter, pl.ds(pl.multiple_of((me % quarter) * part, part), part), :],
        recv_ref.at[:, pl.ds(pl.multiple_of(me * part, part), part), :],
        own_sem,
    )
    own.start()
    fetch.wait()
    load.wait()

    count = per_dev // BLOCK
    for k in range(kinds):
        for u in range(users):
            live = blocks[u] - me * count

            def step(b, carry, k=k, u=u, live=live):
                total, high, low = carry
                x = local[k, u, pl.ds(pl.multiple_of(b * BLOCK, BLOCK), BLOCK), :].astype(jnp.float32)
                x = x.reshape(BLOCK // ROWS, ROWS, width)
                on = b < live
                total = total + jnp.where(on, jnp.sum(x, axis=0), 0.0)
                high = jnp.maximum(high, jnp.where(on, jnp.max(x, axis=0), -jnp.inf))
                low = jnp.minimum(low, jnp.where(on, jnp.min(x, axis=0), jnp.inf))
                return total, high, low

            shape = (ROWS, width)
            total, high, low = lax.fori_loop(
                0, count, step,
                (jnp.zeros(shape, jnp.float32), jnp.full(shape, -jnp.inf, jnp.float32),
                 jnp.full(shape, jnp.inf, jnp.float32)),
            )
            stats_ref[me, 0, k, u, :] = jnp.sum(total, axis=0)
            stats_ref[me, 1, k, u, :] = jnp.max(high, axis=0)
            stats_ref[me, 2, k, u, :] = jnp.min(low, axis=0)

    for d in range(n):
        @pl.when(me != d)
        def _():
            stat(me, d).start()
    for dist in range(2, n):
        start_bulk(dist)

    for s in range(n):
        @pl.when(me != s)
        def _():
            stat(s, me).wait_recv()
    for u in range(users):
        length = (blocks[u] * BLOCK).astype(jnp.float32)
        for k in range(kinds):
            total = stats_ref[0, 0, k, u, :]
            high, low = stats_ref[0, 1, k, u, :], stats_ref[0, 2, k, u, :]
            for s in range(1, n):
                total = total + stats_ref[s, 0, k, u, :]
                high = jnp.maximum(high, stats_ref[s, 1, k, u, :])
                low = jnp.minimum(low, stats_ref[s, 2, k, u, :])
            center = total / jnp.full_like(total, length)
            scale = jnp.maximum(high - center, center - low) + EPSILON
            centers_ref[k, u, :] = center
            scales_ref[k, u, :] = scale
            inverse_ref[k, u, :] = 1.0 / scale

    user = me // quarter
    base = (me % quarter) * part
    length = jnp.zeros((1, width), jnp.int32)
    for u in range(users):
        length = jnp.where(user == u, blocks[u] * BLOCK, length)

    length_ref[...] = length

    def normalise(source, k):
        center = centers_ref[k, pl.ds(user, 1), :]
        inverse = inverse_ref[k, pl.ds(user, 1), :]

        def step(i, _):
            rows = pl.ds(pl.multiple_of(source * part + i * chunk, chunk), chunk)
            first = source * per_dev + base + i * chunk
            recv_ref[k, rows, :] = normalised(recv_ref, k, rows, first, length, center, inverse)
            return 0

        lax.fori_loop(0, part // chunk, step, 0)

    own.wait()
    for k in range(kinds):
        normalise(me, k)
    last = last_source(me, n)
    for dist in range(1, n):
        for source, inside in ((me + dist, me + dist < n), (me - dist, me - dist >= 0)):
            for k in range(kinds):
                @pl.when(inside & (source != last))
                def _():
                    bulk(source, me, k).wait_recv()
                    normalise(source, k)
    for k in range(kinds):
        bulk(last, me, k).wait_recv()
    for s in range(n):
        @pl.when(me != s)
        def _():
            stat(me, s).wait_send()
            for k in range(kinds):
                bulk(me, s, k).wait_send()


def finish(n, quarter, chunk, length_ref, recv_ref, c_ref, s_ref, i_ref, out_ref, centers_ref,
           scales_ref, ready, out_sem, ready_sem, small_sem):
    kinds, positions, width = recv_ref.shape
    part = positions // n
    me = lax.axis_index("seq")
    last = last_source(me, n)

    def place(s, k):
        rows = pl.ds(pl.multiple_of(s * part, part), part)
        return pltpu.make_async_copy(recv_ref.at[k, rows, :], out_ref.at[k, rows, :],
                                     out_sem.at[s, k])

    for s in range(n):
        @pl.when(s != last)
        def _():
            for k in range(kinds):
                place(s, k).start()

    small = [
        pltpu.make_async_copy(c_ref, centers_ref, small_sem.at[0]),
        pltpu.make_async_copy(s_ref, scales_ref, small_sem.at[1]),
    ]
    for copy in small:
        copy.start()

    user = me // quarter
    length = length_ref[...]
    first = last * part * quarter + (me % quarter) * part
    steps = part // chunk

    def late(k, i):
        return pltpu.make_async_copy(
            ready.at[k, pl.ds(i * chunk, chunk), :],
            out_ref.at[k, pl.ds(pl.multiple_of(last * part + i * chunk, chunk), chunk), :],
            ready_sem.at[k, i],
        )

    for k in range(kinds):
        center = c_ref[k, pl.ds(user, 1), :]
        inverse = i_ref[k, pl.ds(user, 1), :]
        for i in range(steps):
            rows = pl.ds(pl.multiple_of(last * part + i * chunk, chunk), chunk)
            ready[k, pl.ds(i * chunk, chunk), :] = normalised(
                recv_ref, k, rows, first + i * chunk, length, center, inverse
            )
            late(k, i).start()
    for copy in small:
        copy.wait()
    for k in range(kinds):
        for i in range(steps):
            late(k, i).wait()
    for s in range(n):
        @pl.when(s != last)
        def _():
            for k in range(kinds):
                place(s, k).wait()


def on_device(kv_cache, valid_blocks):
    kind_count, layer_dev, user_count, per_dev, heads_dev, width = kv_cache.shape
    n = lax.axis_size("seq")
    quarter = n // user_count
    part = per_dev // quarter
    kinds = kind_count * layer_dev * heads_dev
    kv = jnp.transpose(kv_cache, (0, 1, 4, 2, 3, 5)).reshape(kinds, user_count, per_dev, width)
    kv = pltpu.with_memory_space_constraint(kv, pltpu.HBM)
    blocks = pltpu.with_memory_space_constraint(valid_blocks, pltpu.HBM)
    vmem = pl.BlockSpec(memory_space=pltpu.VMEM)
    smem = pl.BlockSpec(memory_space=pltpu.SMEM)
    anywhere = pl.BlockSpec(memory_space=pl.ANY)
    hbm = pl.BlockSpec(memory_space=pltpu.HBM)
    chunk = min(part, CHUNK)
    small = jax.ShapeDtypeStruct((kinds, user_count, width), jnp.float32)
    recv, centers, scales, inverse, length = pl.pallas_call(
        functools.partial(transport, n, quarter, chunk),
        out_shape=(
            jax.ShapeDtypeStruct((kinds, n * part, width), jnp.bfloat16),
            small,
            small,
            small,
            jax.ShapeDtypeStruct((1, width), jnp.int32),
        ),
        in_specs=[hbm, hbm],
        out_specs=(vmem,) * 5,
        scratch_shapes=[
            pltpu.VMEM((n, 3, kinds, user_count, width), jnp.float32),
            pltpu.SMEM((user_count,), jnp.int32),
            pltpu.VMEM((kinds, user_count, per_dev, width), jnp.bfloat16),
            pltpu.SemaphoreType.DMA,
            pltpu.SemaphoreType.DMA,
            pltpu.SemaphoreType.DMA,
            pltpu.SemaphoreType.DMA((n, kinds)),
            pltpu.SemaphoreType.DMA((n, kinds)),
            pltpu.SemaphoreType.DMA((n,)),
            pltpu.SemaphoreType.DMA((n,)),
        ],
        compiler_params=pltpu.CompilerParams(
            collective_id=0, has_side_effects=True, vmem_limit_bytes=GRANT
        ),
        name="transport",
    )(blocks, kv)
    out, centers, scales = pl.pallas_call(
        functools.partial(finish, n, quarter, chunk),
        out_shape=(jax.ShapeDtypeStruct((kinds, n * part, width), jnp.bfloat16), small, small),
        in_specs=[vmem] * 5,
        out_specs=(anywhere, anywhere, anywhere),
        scratch_shapes=[
            pltpu.VMEM((kinds, part, width), jnp.bfloat16),
            pltpu.SemaphoreType.DMA((n, kinds)),
            pltpu.SemaphoreType.DMA((kinds, part // chunk)),
            pltpu.SemaphoreType.DMA((2,)),
        ],
        compiler_params=pltpu.CompilerParams(vmem_limit_bytes=GRANT),
        name="finish",
    )(length, recv, centers, scales, inverse)

    def spread(x, middle):
        x = x.reshape(kind_count, layer_dev, heads_dev, *middle, width)
        return jnp.moveaxis(x, 2, -2)

    return (
        spread(out, (1, n * part)),
        spread(centers, (user_count,)),
        spread(scales, (user_count,)),
    )


def solution(mesh):
    in_specs = (P(None, "layer", "groups", "seq", "head", None), P("groups"))
    out_specs = (
        P(None, "layer", ("groups", "seq"), None, "head", None),
        P(None, "layer", "groups", "head", None),
        P(None, "layer", "groups", "head", None),
    )
    return jax.shard_map(
        on_device, mesh=mesh, in_specs=in_specs, out_specs=out_specs, check_vma=False
    )
```

profile of v0, /device:TPU:0, one launch (start us, length us, event | category | flops | bytes accessed | tf_op | source)
XLA Modules:
  0.0 54.9 jit_solution(3724125999904151635)
XLA Ops:
  0.6 52.7 %transport.1 = (bf16[2,4096,128]{2,1,0:T(8,128)(2,1)S(1)}, f32[2,4,128]{2,1,0:T(4,128)S(1)}, f32[2,4,128]{2,1,0:T(4,128)S(1)}, f32[2,4,128]{2,1,0:T(4,128)S(1)}, s32[1,128]{1,0:T(1,128)S(1)}) custom-call(s32[4]{0:T(128)} %blocks_ref.1, bf16[2,4,1024,128]{3,2,1,0:T(8,128)(2,1)} %bitcast.10), custom_call_target="tpu_custom_call" | custom-call | tf_op jit(solution)/shard_map/transport/pallas_call | solution.py:250
  53.4 1.5 %finish.1 = (bf16[2,4096,128]{2,1,0:T(8,128)(2,1)}, f32[2,4,128]{2,1,0:T(4,128)}, f32[2,4,128]{2,1,0:T(4,128)}) custom-call(s32[1,128]{1,0:T(1,128)S(1)} %get-tuple-element.11.length_ref, bf16[2,4096,128]{2,1,0:T(8,128)(2,1)S(1)} %get-tuple-element.12.recv_ref, f32[2,4,128]{2,1,0:T(4,128)S(1)} %get-tuple-element.13.c_ref, ...), custom_call_target="tpu_custom_call" | custom-call | tf_op jit(solution)/shard_map/finish/pallas_call | solution.py:278
where the time goes:
time: 55 us; the launch traced here: 54.9 us
  Pallas kernels  54.2 us (99%)
  between operations  0.64 us (1%)
    pallas_call x1, Pallas kernels, on_device(): pl.pallas_call(functools.partial(transport, n, quarter, chunk), out_shape...  52.7 us
    pallas_call x1, Pallas kernels, on_device(): pl.pallas_call(functools.partial(finish, n, quarter, chunk), out_shape=(j...  1.48 us

commit v1 on v0

v1 whole, which is shorter than its diff:
```python
import functools

import jax
import jax.numpy as jnp
from jax import lax
from jax.experimental import pallas as pl
from jax.experimental.pallas import tpu as pltpu
from jax.sharding import PartitionSpec as P

BLOCK = 128
ROWS = 8
CHUNK = 256
GRANT = 16 * 2**20
EPSILON = 1e-06


def normalised(recv_ref, k, rows, first, length, center, inverse):
    x = recv_ref[k, rows, :].astype(jnp.float32)
    position = first + lax.broadcasted_iota(jnp.int32, x.shape, 0)
    return jnp.where(position < length, (x - center) * inverse, 0.0).astype(jnp.bfloat16)


def transport(n, quarter, chunk, blocks_ref, kv_ref, recv_ref, centers_ref, scales_ref,
              inverse_ref, stats_ref, blocks, local, load_sem, blocks_sem, own_sem, send_sem, recv_sem,
              stat_send, stat_recv, ready):
    kinds, users, per_dev, width = kv_ref.shape
    part = per_dev // quarter
    pieces = part // chunk
    me = lax.axis_index("seq")
    mids = (n // 2 - 1, n // 2)
    mid = (me == mids[0]) | (me == mids[1])
    outer = (me < mids[0]) | (me > mids[1])

    load = pltpu.make_async_copy(kv_ref, local, load_sem)
    load.start()
    fetch = pltpu.make_async_copy(blocks_ref, blocks, blocks_sem)
    fetch.start()

    barrier = pltpu.get_barrier_semaphore()
    for d in range(n):
        greets = (mid if d in mids else me >= 0) & (me != d)

        @pl.when(greets)
        def _():
            pl.semaphore_signal(barrier, inc=1, device_id={"seq": d})

    @pl.when(mid)
    def _():
        pl.semaphore_wait(barrier, 1)

    @pl.when(outer)
    def _():
        pl.semaphore_wait(barrier, n - 1)
        for d in mids:
            pl.semaphore_signal(ready, inc=1, device_id={"seq": d})

    def bulk(source, target, k, i):
        user, q = target // quarter, target % quarter
        return pltpu.make_async_remote_copy(
            src_ref=kv_ref.at[k, user, pl.ds(pl.multiple_of(q * part + i * chunk, chunk), chunk), :],
            dst_ref=recv_ref.at[k, pl.ds(pl.multiple_of(source * part + i * chunk, chunk), chunk), :],
            send_sem=send_sem.at[target, k, i],
            recv_sem=recv_sem.at[source, k, i],
            device_id={"seq": target},
        )

    def stat(source, target):
        return pltpu.make_async_remote_copy(
            src_ref=stats_ref.at[source],
            dst_ref=stats_ref.at[source],
            send_sem=stat_send.at[target],
            recv_sem=stat_recv.at[source],
            device_id={"seq": target},
        )

    def start_bulk(target, k):
        for i in range(pieces):
            bulk(me, target, k, i).start()

    early = jnp.where(mid, n - 1 - me, jnp.where(me < mids[0], n - 1, 0))
    start_bulk(early, 0)

    own = pltpu.make_async_copy(
        kv_ref.at[:, me // quarter, pl.ds(pl.multiple_of((me % quarter) * part, part), part), :],
        recv_ref.at[:, pl.ds(pl.multiple_of(me * part, part), part), :],
        own_sem,
    )
    own.start()
    fetch.wait()
    load.wait()

    count = per_dev // BLOCK
    for k in range(kinds):
        for u in range(users):
            live = blocks[u] - me * count

            def step(b, carry, k=k, u=u, live=live):
                total, high, low = carry
                x = local[k, u, pl.ds(pl.multiple_of(b * BLOCK, BLOCK), BLOCK), :].astype(jnp.float32)
                x = x.reshape(BLOCK // ROWS, ROWS, width)
                on = b < live
                total = total + jnp.where(on, jnp.sum(x, axis=0), 0.0)
                high = jnp.maximum(high, jnp.where(on, jnp.max(x, axis=0), -jnp.inf))
                low = jnp.minimum(low, jnp.where(on, jnp.min(x, axis=0), jnp.inf))
                return total, high, low

            shape = (ROWS, width)
            total, high, low = lax.fori_loop(
                0, count, step,
                (jnp.zeros(shape, jnp.float32), jnp.full(shape, -jnp.inf, jnp.float32),
                 jnp.full(shape, jnp.inf, jnp.float32)),
            )
            stats_ref[me, 0, k, u, :] = jnp.sum(total, axis=0)
            stats_ref[me, 1, k, u, :] = jnp.max(high, axis=0)
            stats_ref[me, 2, k, u, :] = jnp.min(low, axis=0)

    if n > 2:
        @pl.when(mid)
        def _():
            pl.semaphore_wait(ready, n - 2)

    for d in range(n):
        @pl.when(me != d)
        def _():
            stat(me, d).start()
    for dist in range(n - 1, 0, -1):
        for target, inside in ((me + dist, me + dist < n), (me - dist, me - dist >= 0)):
            for k in range(kinds):
                wanted = inside & (target != early) if k == 0 else inside

                @pl.when(wanted)
                def _():
                    start_bulk(target, k)

    for s in range(n):
        @pl.when(me != s)
        def _():
            stat(s, me).wait_recv()
    for u in range(users):
        length = (blocks[u] * BLOCK).astype(jnp.float32)
        for k in range(kinds):
            total = stats_ref[0, 0, k, u, :]
            high, low = stats_ref[0, 1, k, u, :], stats_ref[0, 2, k, u, :]
            for s in range(1, n):
                total = total + stats_ref[s, 0, k, u, :]
                high = jnp.maximum(high, stats_ref[s, 1, k, u, :])
                low = jnp.minimum(low, stats_ref[s, 2, k, u, :])
            center = total / jnp.full_like(total, length)
            scale = jnp.maximum(high - center, center - low) + EPSILON
            centers_ref[k, u, :] = center
            scales_ref[k, u, :] = scale
            inverse_ref[k, u, :] = 1.0 / scale

    user = me // quarter
    base = (me % quarter) * part
    length = jnp.zeros((1, width), jnp.int32)
    for u in range(users):
        length = jnp.where(user == u, blocks[u] * BLOCK, length)

    def normalise(source, k, i):
        center = centers_ref[k, pl.ds(user, 1), :]
        inverse = inverse_ref[k, pl.ds(user, 1), :]
        rows = pl.ds(pl.multiple_of(source * part + i * chunk, chunk), chunk)
        first = source * per_dev + base + i * chunk
        recv_ref[k, rows, :] = normalised(recv_ref, k, rows, first, length, center, inverse)

    def arrive(source, k):
        def step(i, _):
            bulk(source, me, k, i).wait_recv()
            normalise(source, k, i)
            return 0

        lax.fori_loop(0, pieces, step, 0)

    own.wait()
    for k in range(kinds):
        def step(i, _, k=k):
            normalise(me, k, i)
            return 0

        lax.fori_loop(0, pieces, step, 0)
    for dist in range(n - 1, 0, -1):
        for source, inside in ((me + dist, me + dist < n), (me - dist, me - dist >= 0)):
            late = mid & (source == n - 1 - me) if dist == 1 else me < 0
            for k in range(kinds):
                @pl.when(inside & ~late)
                def _():
                    arrive(source, k)

    @pl.when(mid)
    def _():
        for k in range(kinds):
            arrive(n - 1 - me, k)

    for s in range(n):
        @pl.when(me != s)
        def _():
            stat(me, s).wait_send()
            for k in range(kinds):
                for i in range(pieces):
                    bulk(me, s, k, i).wait_send()


def finish(recv_ref, c_ref, s_ref, out_ref, centers_ref, scales_ref, sems):
    copies = [
        pltpu.make_async_copy(recv_ref, out_ref, sems.at[0]),
        pltpu.make_async_copy(c_ref, centers_ref, sems.at[1]),
        pltpu.make_async_copy(s_ref, scales_ref, sems.at[2]),
    ]
    for copy in copies:
        copy.start()
    for copy in copies:
        copy.wait()


def on_device(kv_cache, valid_blocks):
    kind_count, layer_dev, user_count, per_dev, heads_dev, width = kv_cache.shape
    n = lax.axis_size("seq")
    quarter = n // user_count
    part = per_dev // quarter
    kinds = kind_count * layer_dev * heads_dev
    kv = jnp.transpose(kv_cache, (0, 1, 4, 2, 3, 5)).reshape(kinds, user_count, per_dev, width)
    kv = pltpu.with_memory_space_constraint(kv, pltpu.HBM)
    blocks = pltpu.with_memory_space_constraint(valid_blocks, pltpu.HBM)
    vmem = pl.BlockSpec(memory_space=pltpu.VMEM)
    smem = pl.BlockSpec(memory_space=pltpu.SMEM)
    anywhere = pl.BlockSpec(memory_space=pl.ANY)
    hbm = pl.BlockSpec(memory_space=pltpu.HBM)
    chunk = min(part, CHUNK)
    small = jax.ShapeDtypeStruct((kinds, user_count, width), jnp.float32)
    recv, centers, scales = pl.pallas_call(
        functools.partial(transport, n, quarter, chunk),
        out_shape=(
            jax.ShapeDtypeStruct((kinds, n * part, width), jnp.bfloat16),
            small,
            small,
        ),
        in_specs=[hbm, hbm],
        out_specs=(vmem,) * 3,
        scratch_shapes=[
            pltpu.VMEM((kinds, user_count, width), jnp.float32),
            pltpu.VMEM((n, 3, kinds, user_count, width), jnp.float32),
            pltpu.SMEM((user_count,), jnp.int32),
            pltpu.VMEM((kinds, user_count, per_dev, width), jnp.bfloat16),
            pltpu.SemaphoreType.DMA,
            pltpu.SemaphoreType.DMA,
            pltpu.SemaphoreType.DMA,
            pltpu.SemaphoreType.DMA((n, kinds, part // chunk)),
            pltpu.SemaphoreType.DMA((n, kinds, part // chunk)),
            pltpu.SemaphoreType.DMA((n,)),
            pltpu.SemaphoreType.DMA((n,)),
            pltpu.SemaphoreType.REGULAR,
        ],
        compiler_params=pltpu.CompilerParams(
            collective_id=0, has_side_effects=True, vmem_limit_bytes=GRANT
        ),
        name="transport",
    )(blocks, kv)
    out, centers, scales = pl.pallas_call(
        finish,
        out_shape=(jax.ShapeDtypeStruct((kinds, n * part, width), jnp.bfloat16), small, small),
        in_specs=[vmem] * 3,
        out_specs=(anywhere, anywhere, anywhere),
        scratch_shapes=[pltpu.SemaphoreType.DMA((3,))],
        compiler_params=pltpu.CompilerParams(vmem_limit_bytes=GRANT),
        name="finish",
    )(recv, centers, scales)

    def spread(x, middle):
        x = x.reshape(kind_count, layer_dev, heads_dev, *middle, width)
        return jnp.moveaxis(x, 2, -2)

    return (
        spread(out, (1, n * part)),
        spread(centers, (user_count,)),
        spread(scales, (user_count,)),
    )


def solution(mesh):
    in_specs = (P(None, "layer", "groups", "seq", "head", None), P("groups"))
    out_specs = (
        P(None, "layer", ("groups", "seq"), None, "head", None),
        P(None, "layer", "groups", "head", None),
        P(None, "layer", "groups", "head", None),
    )
    return jax.shard_map(
        on_device, mesh=mesh, in_specs=in_specs, out_specs=out_specs, check_vma=False
    )
```

time: 55 us -> 51.6 us (0.938)
  the two profiles are of different devices: /device:TPU:0 before, /device:TPU:12 now
where the time goes in v1:
time: 51.6 us; the launch traced here: 51.4 us
  Pallas kernels  50.8 us (98%)
  between operations  0.64 us (1%)
    pallas_call x1, Pallas kernels, on_device(): pl.pallas_call(functools.partial(transport, n, quarter, chunk), out_shape...  49.5 us
    pallas_call x1, Pallas kernels, on_device(): pl.pallas_call(finish, out_shape=(jax.ShapeDtypeStruct((kinds, n * part,...  1.35 us

profile of v1, /device:TPU:12, one launch (start us, length us, event | category | flops | bytes accessed | tf_op | source)
XLA Modules:
  0.0 51.4 jit_solution(2474320977822635118)
XLA Ops:
  0.6 49.5 %transport.1 = (bf16[2,4096,128]{2,1,0:T(8,128)(2,1)S(1)}, f32[2,4,128]{2,1,0:T(4,128)S(1)}, f32[2,4,128]{2,1,0:T(4,128)S(1)}) custom-call(s32[4]{0:T(128)} %blocks_ref.1, bf16[2,4,1024,128]{3,2,1,0:T(8,128)(2,1)} %bitcast.10), custom_call_target="tpu_custom_call" | custom-call | tf_op jit(solution)/shard_map/transport/pallas_call | solution.py:231
  50.1 1.4 %finish.1 = (bf16[2,4096,128]{2,1,0:T(8,128)(2,1)}, f32[2,4,128]{2,1,0:T(4,128)}, f32[2,4,128]{2,1,0:T(4,128)}) custom-call(bf16[2,4096,128]{2,1,0:T(8,128)(2,1)S(1)} %get-tuple-element.9.recv_ref, f32[2,4,128]{2,1,0:T(4,128)S(1)} %get-tuple-element.10.c_ref, f32[2,4,128]{2,1,0:T(4,128)S(1)} %get-tuple-element.11.s_ref), custom_call_target="tpu_custom_call" | custom-call | tf_op jit(solution)/shard_map/finish/pallas_call | solution.py:259

commit v2 on v1

--- a/solution.py
+++ b/solution.py
@@ -9,7 +9,7 @@
 
 BLOCK = 128
 ROWS = 8
-CHUNK = 256
+CHUNK = 512
 GRANT = 16 * 2**20
 EPSILON = 1e-06
 
@@ -21,8 +21,8 @@
 
 
 def transport(n, quarter, chunk, blocks_ref, kv_ref, recv_ref, centers_ref, scales_ref,
-              inverse_ref, stats_ref, blocks, local, load_sem, blocks_sem, own_sem, send_sem, recv_sem,
-              stat_send, stat_recv, ready):
+              inverse_ref, stats_ref, half_ref, full_ref, blocks, local, load_sem, blocks_sem, own_sem, send_sem, recv_sem,
+              stat_send, stat_recv, half_send, half_recv, full_send, full_recv, ready):
     kinds, users, per_dev, width = kv_ref.shape
     part = per_dev // quarter
     pieces = part // chunk
@@ -30,6 +30,7 @@
     mids = (n // 2 - 1, n // 2)
     mid = (me == mids[0]) | (me == mids[1])
     outer = (me < mids[0]) | (me > mids[1])
+    side = me // (n // 2)
 
     load = pltpu.make_async_copy(kv_ref, local, load_sem)
     load.start()
@@ -68,17 +69,45 @@
         return pltpu.make_async_remote_copy(
             src_ref=stats_ref.at[source],
             dst_ref=stats_ref.at[source],
-            send_sem=stat_send.at[target],
+            send_sem=stat_send,
             recv_sem=stat_recv.at[source],
             device_id={"seq": target},
         )
 
-    def start_bulk(target, k):
-        for i in range(pieces):
+    def across(origin):
+        return pltpu.make_async_remote_copy(
+            src_ref=half_ref.at[origin],
+            dst_ref=half_ref.at[origin],
+            send_sem=half_send,
+            recv_sem=half_recv,
+            device_id={"seq": n - 1 - me},
+        )
+
+    def handed(target):
+        return pltpu.make_async_remote_copy(
+            src_ref=full_ref,
+            dst_ref=full_ref,
+            send_sem=full_send.at[target],
+            recv_sem=full_recv,
+            device_id={"seq": target},
+        )
+
+    def start_bulk(target, k, chunks):
+        for i in chunks:
             bulk(me, target, k, i).start()
 
+    def combine(into, left, right):
+        into[0] = left[0] + right[0]
+        into[1] = jnp.maximum(left[1], right[1])
+        into[2] = jnp.minimum(left[2], right[2])
+
     early = jnp.where(mid, n - 1 - me, jnp.where(me < mids[0], n - 1, 0))
-    start_bulk(early, 0)
+    start_bulk(early, 0, range(1))
+
+    @pl.when(outer)
+    def _():
+        start_bulk(early, 0, range(1, pieces))
+
 
     own = pltpu.make_async_copy(
         kv_ref.at[:, me // quarter, pl.ds(pl.multiple_of((me % quarter) * part, part), part), :],
@@ -114,37 +143,54 @@
             stats_ref[me, 1, k, u, :] = jnp.max(high, axis=0)
             stats_ref[me, 2, k, u, :] = jnp.min(low, axis=0)
 
-    if n > 2:
-        @pl.when(mid)
-        def _():
-            pl.semaphore_wait(ready, n - 2)
-
-    for d in range(n):
-        @pl.when(me != d)
-        def _():
-            stat(me, d).start()
+    for h in range(2):
+        @pl.when(outer & (side == h))
+        def _():
+            stat(me, mids[h]).start()
+
+        @pl.when(mid & (side == h))
+        def _():
+            if n > 2:
+                pl.semaphore_wait(ready, n - 2)
+            inner = [s for s in range(n) if s // (n // 2) == h and s != mids[h]]
+            half_ref[h] = stats_ref[mids[h]]
+            for s in inner:
+                stat(s, me).wait_recv()
+                combine(half_ref.at[h], half_ref.at[h], stats_ref.at[s])
+            across(h).start()
+
     for dist in range(n - 1, 0, -1):
         for target, inside in ((me + dist, me + dist < n), (me - dist, me - dist >= 0)):
-            for k in range(kinds):
-                wanted = inside & (target != early) if k == 0 else inside
-
-                @pl.when(wanted)
-                def _():
-                    start_bulk(target, k)
-
-    for s in range(n):
-        @pl.when(me != s)
-        def _():
-            stat(s, me).wait_recv()
+            @pl.when(inside & (target != early))
+            def _():
+                start_bulk(target, 0, range(pieces))
+
+            @pl.when(inside & (target == early) & mid)
+            def _():
+                start_bulk(target, 0, range(1, pieces))
+
+            @pl.when(inside)
+            def _():
+                for k in range(1, kinds):
+                    start_bulk(target, k, range(pieces))
+
+    for h in range(2):
+        @pl.when(mid & (side == h))
+        def _():
+            across(1 - h).wait_recv()
+            combine(full_ref, half_ref.at[0], half_ref.at[1])
+            for s in range(n):
+                if s // (n // 2) == h and s != mids[h]:
+                    handed(s).start()
+
+    @pl.when(outer)
+    def _():
+        handed(me).wait_recv()
+
     for u in range(users):
         length = (blocks[u] * BLOCK).astype(jnp.float32)
         for k in range(kinds):
-            total = stats_ref[0, 0, k, u, :]
-            high, low = stats_ref[0, 1, k, u, :], stats_ref[0, 2, k, u, :]
-            for s in range(1, n):
-                total = total + stats_ref[s, 0, k, u, :]
-                high = jnp.maximum(high, stats_ref[s, 1, k, u, :])
-                low = jnp.minimum(low, stats_ref[s, 2, k, u, :])
+            total, high, low = full_ref[0, k, u, :], full_ref[1, k, u, :], full_ref[2, k, u, :]
             center = total / jnp.full_like(total, length)
             scale = jnp.maximum(high - center, center - low) + EPSILON
             centers_ref[k, u, :] = center
@@ -195,10 +241,21 @@
     for s in range(n):
         @pl.when(me != s)
         def _():
-            stat(me, s).wait_send()
             for k in range(kinds):
                 for i in range(pieces):
                     bulk(me, s, k, i).wait_send()
+
+    for h in range(2):
+        @pl.when(outer & (side == h))
+        def _():
+            stat(me, mids[h]).wait_send()
+
+        @pl.when(mid & (side == h))
+        def _():
+            across(h).wait_send()
+            for s in range(n):
+                if s // (n // 2) == h and s != mids[h]:
+                    handed(s).wait_send()
 
 
 def finish(recv_ref, c_ref, s_ref, out_ref, centers_ref, scales_ref, sems):
@@ -240,6 +297,8 @@
         scratch_shapes=[
             pltpu.VMEM((kinds, user_count, width), jnp.float32),
             pltpu.VMEM((n, 3, kinds, user_count, width), jnp.float32),
+            pltpu.VMEM((2, 3, kinds, user_count, width), jnp.float32),
+            pltpu.VMEM((3, kinds, user_count, width), jnp.float32),
             pltpu.SMEM((user_count,), jnp.int32),
             pltpu.VMEM((kinds, user_count, per_dev, width), jnp.bfloat16),
             pltpu.SemaphoreType.DMA,
@@ -247,8 +306,12 @@
             pltpu.SemaphoreType.DMA,
             pltpu.SemaphoreType.DMA((n, kinds, part // chunk)),
             pltpu.SemaphoreType.DMA((n, kinds, part // chunk)),
+            pltpu.SemaphoreType.DMA,
             pltpu.SemaphoreType.DMA((n,)),
+            pltpu.SemaphoreType.DMA,
+            pltpu.SemaphoreType.DMA,
             pltpu.SemaphoreType.DMA((n,)),
+            pltpu.SemaphoreType.DMA,
             pltpu.SemaphoreType.REGULAR,
         ],
         compiler_params=pltpu.CompilerParams(

time: 51.6 us -> 50.6 us (0.981)
  Pallas kernels: 50.8 us -> 49.8 us
    pallas_call x1, Pallas kernels: 49.5 us -> 48.5 us  [on_device(): pl.pallas_call(functools.partial(transport, n, quarter, chunk), out_shape...]
where the time goes in v2:
time: 50.6 us; the launch traced here: 50.5 us
  Pallas kernels  49.8 us (98%)
  between operations  0.64 us (1%)
    pallas_call x1, Pallas kernels, on_device(): pl.pallas_call(functools.partial(transport, n, quarter, chunk), out_shape...  48.5 us
    pallas_call x1, Pallas kernels, on_device(): pl.pallas_call(finish, out_shape=(jax.ShapeDtypeStruct((kinds, n * part,...  1.35 us

profile of v2, /device:TPU:12, one launch (start us, length us, event | category | flops | bytes accessed | tf_op | source)
XLA Modules:
  0.0 50.5 jit_solution(11629329800108994204)
XLA Ops:
  0.6 48.5 %transport.1 = (bf16[2,4096,128]{2,1,0:T(8,128)(2,1)S(1)}, f32[2,4,128]{2,1,0:T(4,128)S(1)}, f32[2,4,128]{2,1,0:T(4,128)S(1)}) custom-call(s32[4]{0:T(128)} %blocks_ref.1, bf16[2,4,1024,128]{3,2,1,0:T(8,128)(2,1)} %bitcast.10), custom_call_target="tpu_custom_call" | custom-call | tf_op jit(solution)/shard_map/transport/pallas_call | solution.py:288
  49.1 1.4 %finish.1 = (bf16[2,4096,128]{2,1,0:T(8,128)(2,1)}, f32[2,4,128]{2,1,0:T(4,128)}, f32[2,4,128]{2,1,0:T(4,128)}) custom-call(bf16[2,4096,128]{2,1,0:T(8,128)(2,1)S(1)} %get-tuple-element.9.recv_ref, f32[2,4,128]{2,1,0:T(4,128)S(1)} %get-tuple-element.10.c_ref, f32[2,4,128]{2,1,0:T(4,128)S(1)} %get-tuple-element.11.s_ref), custom_call_target="tpu_custom_call" | custom-call | tf_op jit(solution)/shard_map/finish/pallas_call | solution.py:322

commit v3 on v2

--- a/solution.py
+++ b/solution.py
@@ -9,7 +9,6 @@
 
 BLOCK = 128
 ROWS = 8
-CHUNK = 512
 GRANT = 16 * 2**20
 EPSILON = 1e-06
 
@@ -20,12 +19,13 @@
     return jnp.where(position < length, (x - center) * inverse, 0.0).astype(jnp.bfloat16)
 
 
-def transport(n, quarter, chunk, blocks_ref, kv_ref, recv_ref, centers_ref, scales_ref,
-              inverse_ref, stats_ref, half_ref, full_ref, blocks, local, load_sem, blocks_sem, own_sem, send_sem, recv_sem,
+def transport(n, quarter, blocks_ref, kv_ref, recv_ref, centers_ref, scales_ref,
+              inverse_ref, stats_ref, half_ref, full_ref, blocks, local, load_sem, blocks_sem, own_sem, send_sem, recv_sem, pair_send, pair_recv,
               stat_send, stat_recv, half_send, half_recv, full_send, full_recv, ready):
     kinds, users, per_dev, width = kv_ref.shape
     part = per_dev // quarter
-    pieces = part // chunk
+    cuts = (0, 3 * part // 4, part)
+    spans = tuple((a, b - a) for a, b in zip(cuts, cuts[1:]))
     me = lax.axis_index("seq")
     mids = (n // 2 - 1, n // 2)
     mid = (me == mids[0]) | (me == mids[1])
@@ -55,15 +55,25 @@
         for d in mids:
             pl.semaphore_signal(ready, inc=1, device_id={"seq": d})
 
-    def bulk(source, target, k, i):
+    partner = n - 1 - me
+
+    def copy(src, source, target, k, start, rows, sems):
         user, q = target // quarter, target % quarter
+        unit = part // 4
         return pltpu.make_async_remote_copy(
-            src_ref=kv_ref.at[k, user, pl.ds(pl.multiple_of(q * part + i * chunk, chunk), chunk), :],
-            dst_ref=recv_ref.at[k, pl.ds(pl.multiple_of(source * part + i * chunk, chunk), chunk), :],
-            send_sem=send_sem.at[target, k, i],
-            recv_sem=recv_sem.at[source, k, i],
+            src_ref=src.at[k, user, pl.ds(pl.multiple_of(q * part + start, unit), rows), :],
+            dst_ref=recv_ref.at[k, pl.ds(pl.multiple_of(source * part + start, unit), rows), :],
+            send_sem=sems[0],
+            recv_sem=sems[1],
             device_id={"seq": target},
         )
+
+    def bulk(source, target, k, src=local):
+        return copy(src, source, target, k, 0, part, (send_sem.at[target, k], recv_sem.at[source, k]))
+
+    def pair(source, target, k, i, src=local):
+        start, rows = spans[i]
+        return copy(src, source, target, k, start, rows, (pair_send.at[k, i], pair_recv.at[k, i]))
 
     def stat(source, target):
         return pltpu.make_async_remote_copy(
@@ -92,22 +102,20 @@
             device_id={"seq": target},
         )
 
-    def start_bulk(target, k, chunks):
-        for i in chunks:
-            bulk(me, target, k, i).start()
-
     def combine(into, left, right):
         into[0] = left[0] + right[0]
         into[1] = jnp.maximum(left[1], right[1])
         into[2] = jnp.minimum(left[2], right[2])
 
-    early = jnp.where(mid, n - 1 - me, jnp.where(me < mids[0], n - 1, 0))
-    start_bulk(early, 0, range(1))
+    early = jnp.where(me < mids[0], n - 1, 0)
+
+    @pl.when(mid)
+    def _():
+        pair(me, partner, 0, 0, kv_ref).start()
 
     @pl.when(outer)
     def _():
-        start_bulk(early, 0, range(1, pieces))
-
+        bulk(me, early, 0, kv_ref).start()
 
     own = pltpu.make_async_copy(
         kv_ref.at[:, me // quarter, pl.ds(pl.multiple_of((me % quarter) * part, part), part), :],
@@ -161,18 +169,20 @@
 
     for dist in range(n - 1, 0, -1):
         for target, inside in ((me + dist, me + dist < n), (me - dist, me - dist >= 0)):
-            @pl.when(inside & (target != early))
-            def _():
-                start_bulk(target, 0, range(pieces))
-
-            @pl.when(inside & (target == early) & mid)
-            def _():
-                start_bulk(target, 0, range(1, pieces))
-
-            @pl.when(inside)
-            def _():
-                for k in range(1, kinds):
-                    start_bulk(target, k, range(pieces))
+            paired = mid & (target == partner)
+            for k in range(kinds):
+                sent = outer & (target == early) if k == 0 else me < 0
+
+                @pl.when(inside & ~paired & ~sent)
+                def _():
+                    bulk(me, target, k).start()
+
+    @pl.when(mid)
+    def _():
+        for k in range(kinds):
+            for i in range(len(spans)):
+                if k + i > 0:
+                    pair(me, partner, k, i).start()
 
     for h in range(2):
         @pl.when(mid & (side == h))
@@ -203,47 +213,52 @@
     for u in range(users):
         length = jnp.where(user == u, blocks[u] * BLOCK, length)
 
-    def normalise(source, k, i):
+    def normalise(source, k, start, rows):
         center = centers_ref[k, pl.ds(user, 1), :]
         inverse = inverse_ref[k, pl.ds(user, 1), :]
-        rows = pl.ds(pl.multiple_of(source * part + i * chunk, chunk), chunk)
-        first = source * per_dev + base + i * chunk
-        recv_ref[k, rows, :] = normalised(recv_ref, k, rows, first, length, center, inverse)
-
-    def arrive(source, k):
-        def step(i, _):
-            bulk(source, me, k, i).wait_recv()
-            normalise(source, k, i)
+        step = part // 4
+
+        def at(i, _):
+            here = start + i * step
+            place = pl.ds(pl.multiple_of(source * part + here, step), step)
+            first = source * per_dev + base + here
+            recv_ref[k, place, :] = normalised(recv_ref, k, place, first, length, center, inverse)
             return 0
 
-        lax.fori_loop(0, pieces, step, 0)
+        lax.fori_loop(0, rows // step, at, 0)
 
     own.wait()
     for k in range(kinds):
-        def step(i, _, k=k):
-            normalise(me, k, i)
-            return 0
-
-        lax.fori_loop(0, pieces, step, 0)
+        normalise(me, k, 0, part)
     for dist in range(n - 1, 0, -1):
         for source, inside in ((me + dist, me + dist < n), (me - dist, me - dist >= 0)):
-            late = mid & (source == n - 1 - me) if dist == 1 else me < 0
+            paired = mid & (source == partner)
             for k in range(kinds):
-                @pl.when(inside & ~late)
+                @pl.when(inside & ~paired)
                 def _():
-                    arrive(source, k)
+                    bulk(source, me, k).wait_recv()
+                    normalise(source, k, 0, part)
 
     @pl.when(mid)
     def _():
         for k in range(kinds):
-            arrive(n - 1 - me, k)
+            for i, (start, rows) in enumerate(spans):
+                pair(partner, me, k, i).wait_recv()
+                normalise(partner, k, start, rows)
 
     for s in range(n):
-        @pl.when(me != s)
+        paired = mid & (partner == s)
+
+        @pl.when((me != s) & ~paired)
         def _():
             for k in range(kinds):
-                for i in range(pieces):
-                    bulk(me, s, k, i).wait_send()
+                bulk(me, s, k).wait_send()
+
+    @pl.when(mid)
+    def _():
+        for k in range(kinds):
+            for i in range(len(spans)):
+                pair(me, partner, k, i).wait_send()
 
     for h in range(2):
         @pl.when(outer & (side == h))
@@ -283,10 +298,9 @@
     smem = pl.BlockSpec(memory_space=pltpu.SMEM)
     anywhere = pl.BlockSpec(memory_space=pl.ANY)
     hbm = pl.BlockSpec(memory_space=pltpu.HBM)
-    chunk = min(part, CHUNK)
     small = jax.ShapeDtypeStruct((kinds, user_count, width), jnp.float32)
     recv, centers, scales = pl.pallas_call(
-        functools.partial(transport, n, quarter, chunk),
+        functools.partial(transport, n, quarter),
         out_shape=(
             jax.ShapeDtypeStruct((kinds, n * part, width), jnp.bfloat16),
             small,
@@ -304,8 +318,10 @@
             pltpu.SemaphoreType.DMA,
             pltpu.SemaphoreType.DMA,
             pltpu.SemaphoreType.DMA,
-            pltpu.SemaphoreType.DMA((n, kinds, part // chunk)),
-            pltpu.SemaphoreType.DMA((n, kinds, part // chunk)),
+            pltpu.SemaphoreType.DMA((n, kinds)),
+            pltpu.SemaphoreType.DMA((n, kinds)),
+            pltpu.SemaphoreType.DMA((kinds, 2)),
+            pltpu.SemaphoreType.DMA((kinds, 2)),
             pltpu.SemaphoreType.DMA,
             pltpu.SemaphoreType.DMA((n,)),
             pltpu.SemaphoreType.DMA,

time: 50.6 us -> 50.5 us (level)
  no operation moved by 1% of the time
where the time goes in v3:
time: 50.5 us; the launch traced here: 50.4 us
  Pallas kernels  49.7 us (98%)
  between operations  0.64 us (1%)
    pallas_call x1, Pallas kernels, on_device(): pl.pallas_call(functools.partial(transport, n, quarter), out_shape=(jax.S...  48.4 us
    pallas_call x1, Pallas kernels, on_device(): pl.pallas_call(finish, out_shape=(jax.ShapeDtypeStruct((kinds, n * part,...  1.35 us

profile of v3, /device:TPU:12, one launch (start us, length us, event | category | flops | bytes accessed | tf_op | source)
XLA Modules:
  0.0 50.4 jit_solution(6198815780935982359)
XLA Ops:
  0.6 48.4 %transport.1 = (bf16[2,4096,128]{2,1,0:T(8,128)(2,1)S(1)}, f32[2,4,128]{2,1,0:T(4,128)S(1)}, f32[2,4,128]{2,1,0:T(4,128)S(1)}) custom-call(s32[4]{0:T(128)} %blocks_ref.1, bf16[2,4,1024,128]{3,2,1,0:T(8,128)(2,1)} %bitcast.10), custom_call_target="tpu_custom_call" | custom-call | tf_op jit(solution)/shard_map/transport/pallas_call | solution.py:302
  49.0 1.4 %finish.1 = (bf16[2,4096,128]{2,1,0:T(8,128)(2,1)}, f32[2,4,128]{2,1,0:T(4,128)}, f32[2,4,128]{2,1,0:T(4,128)}) custom-call(bf16[2,4096,128]{2,1,0:T(8,128)(2,1)S(1)} %get-tuple-element.9.recv_ref, f32[2,4,128]{2,1,0:T(4,128)S(1)} %get-tuple-element.10.c_ref, f32[2,4,128]{2,1,0:T(4,128)S(1)} %get-tuple-element.11.s_ref), custom_call_target="tpu_custom_call" | custom-call | tf_op jit(solution)/shard_map/finish/pallas_call | solution.py:338

commit v4 on v2

v4 whole, which is shorter than its diff:
```python
import functools

import jax
import jax.numpy as jnp
from jax import lax
from jax.experimental import pallas as pl
from jax.experimental.pallas import tpu as pltpu
from jax.sharding import PartitionSpec as P

BLOCK = 128
ROWS = 8
GRANT = 16 * 2**20
EPSILON = 1e-06
CLASSES = (
    (8, 8, 8, 8),
    (4, 8, 4, 8),
    (8, 4, 8, 4),
    (8, 2, 4, 8),
    (2, 8, 8, 4),
)


def classes(users):
    return tuple(c for c in CLASSES if len(c) == users) or ((8,) * users,)


def normalised(x, first, length, center, inverse):
    x = x.astype(jnp.float32)
    position = first + lax.broadcasted_iota(jnp.int32, x.shape, 0)
    return jnp.where(position < length, (x - center) * inverse, 0.0).astype(jnp.bfloat16)


def combine(into, left, right):
    into[0] = left[0] + right[0]
    into[1] = jnp.maximum(left[1], right[1])
    into[2] = jnp.minimum(left[2], right[2])


def each(low, high, action):
    def step(i, _):
        action(i)
        return 0

    lax.fori_loop(low, high, step, 0)


def gather(n, groups, quarter, blocks_ref, kv_ref, recv_ref, centers_ref, scales_ref, inverse_ref,
           lengths_ref, choice_ref, blocks, local, stats_ref, half_ref, full_ref,
           load_sem, fetch_sem, own_sem, send_sem, recv_sem, cut_send, cut_recv, stat_send, stat_recv,
           half_send, half_recv, full_send, full_recv, swap_send, swap_recv, ready):
    kinds, users, per_dev, width = kv_ref.shape
    part = per_dev // quarter
    half = n // 2
    me = lax.axis_index("seq")
    group = lax.axis_index("groups")
    mids = (half - 1, half)
    ends = (0, n - 1)
    mid = (me == mids[0]) | (me == mids[1])
    outer = (me < mids[0]) | (me > mids[1])
    side = me // half
    partner = n - 1 - me

    load = pltpu.make_async_copy(kv_ref, local, load_sem)
    load.start()
    fetch = pltpu.make_async_copy(blocks_ref, blocks.at[group], fetch_sem)
    fetch.start()

    barrier = pltpu.get_barrier_semaphore()
    for g in range(groups):
        @pl.when(group != g)
        def _():
            pl.semaphore_signal(barrier, inc=1, device_id={"groups": g})
    for d in range(n):
        greets = (mid if d in mids else me >= 0) & (me != d)

        @pl.when(greets)
        def _():
            pl.semaphore_signal(barrier, inc=1, device_id={"seq": d})

    @pl.when(mid)
    def _():
        pl.semaphore_wait(barrier, groups)

    @pl.when(outer)
    def _():
        pl.semaphore_wait(barrier, n + groups - 2)
        for d in mids:
            pl.semaphore_signal(ready, inc=1, device_id={"seq": d})

    def bulk(source, target, k):
        user, q = target // quarter, target % quarter
        return pltpu.make_async_remote_copy(
            src_ref=local.at[k, user, pl.ds(pl.multiple_of(q * part, part), part), :],
            dst_ref=recv_ref.at[k, pl.ds(pl.multiple_of(source * part, part), part), :],
            send_sem=send_sem.at[target, k],
            recv_sem=recv_sem.at[source, k],
            device_id={"seq": target},
        )

    def cut(source, target, k, i, src=local):
        user, q = target // quarter, target % quarter
        rows = part // 2
        return pltpu.make_async_remote_copy(
            src_ref=src.at[k, user, pl.ds(pl.multiple_of(q * part + i * rows, rows), rows), :],
            dst_ref=recv_ref.at[k, pl.ds(pl.multiple_of(source * part + i * rows, rows), rows), :],
            send_sem=cut_send.at[k, i],
            recv_sem=cut_recv.at[source, k, i],
            device_id={"seq": target},
        )

    def stat(source, target):
        return pltpu.make_async_remote_copy(
            src_ref=stats_ref.at[source],
            dst_ref=stats_ref.at[source],
            send_sem=stat_send,
            recv_sem=stat_recv.at[source],
            device_id={"seq": target},
        )

    def across(origin):
        return pltpu.make_async_remote_copy(
            src_ref=half_ref.at[origin],
            dst_ref=half_ref.at[origin],
            send_sem=half_send,
            recv_sem=half_recv,
            device_id={"seq": partner},
        )

    def handed(target):
        return pltpu.make_async_remote_copy(
            src_ref=full_ref,
            dst_ref=full_ref,
            send_sem=full_send.at[target],
            recv_sem=full_recv,
            device_id={"seq": target},
        )

    def swap(origin, g):
        return pltpu.make_async_remote_copy(
            src_ref=blocks.at[origin],
            dst_ref=blocks.at[origin],
            send_sem=swap_send.at[g],
            recv_sem=swap_recv.at[origin],
            device_id={"groups": g},
        )

    @pl.when(outer)
    def _():
        load.wait()

    for h in range(2):
        @pl.when(outer & (side == h))
        def _():
            cut(me, mids[1 - h], 0, 0, kv_ref).start()

    own = pltpu.make_async_copy(
        kv_ref.at[:, me // quarter, pl.ds(pl.multiple_of((me % quarter) * part, part), part), :],
        recv_ref.at[:, pl.ds(pl.multiple_of(me * part, part), part), :],
        own_sem,
    )
    own.start()
    fetch.wait()
    for g in range(groups):
        @pl.when(group != g)
        def _():
            swap(group, g).start()

    @pl.when(mid)
    def _():
        load.wait()

    for u in range(users):
        lengths_ref[pl.ds(u, 1), :] = jnp.full((1, width), blocks[group, u] * BLOCK, jnp.int32)
    count = per_dev // BLOCK
    for k in range(kinds):
        for u in range(users):
            live = blocks[group, u] - me * count

            def step(b, carry, k=k, u=u, live=live):
                total, high, low = carry
                x = local[k, u, pl.ds(pl.multiple_of(b * BLOCK, BLOCK), BLOCK), :].astype(jnp.float32)
                x = x.reshape(BLOCK // ROWS, ROWS, width)
                on = b < live
                total = total + jnp.where(on, jnp.sum(x, axis=0), 0.0)
                high = jnp.maximum(high, jnp.where(on, jnp.max(x, axis=0), -jnp.inf))
                low = jnp.minimum(low, jnp.where(on, jnp.min(x, axis=0), jnp.inf))
                return total, high, low

            shape = (ROWS, width)
            total, high, low = lax.fori_loop(
                0, count, step,
                (jnp.zeros(shape, jnp.float32), jnp.full(shape, -jnp.inf, jnp.float32),
                 jnp.full(shape, jnp.inf, jnp.float32)),
            )
            stats_ref[me, 0, k, u, :] = jnp.sum(total, axis=0)
            stats_ref[me, 1, k, u, :] = jnp.max(high, axis=0)
            stats_ref[me, 2, k, u, :] = jnp.min(low, axis=0)

    if n > 2:
        @pl.when(mid)
        def _():
            pl.semaphore_wait(ready, n - 2)

    odd = lax.axis_index("layer") % 2 == 1

    for h in range(2):
        halves = range(h * half, (h + 1) * half)
        others = [s for s in halves if s != ends[h]]
        there = [s for s in range(n) if s // half != h and s not in mids]

        @pl.when((side == h) & (me != ends[h]))
        def _():
            stat(me, ends[h]).start()

        @pl.when(outer & (me != ends[h]) & (side == h))
        def _():
            for k in range(kinds):
                for i in range(2):
                    if k + i:
                        cut(me, mids[1 - h], k, i).start()

        @pl.when(me == ends[h])
        def _():
            @pl.when(odd)
            def _():
                cut(me, mids[1 - h], 0, 1).start()

            half_ref[h] = stats_ref[ends[h]]
            for s in others:
                stat(s, me).wait_recv()
                combine(half_ref.at[h], half_ref.at[h], stats_ref.at[s])
            across(h).start()

            @pl.when(~odd)
            def _():
                cut(me, mids[1 - h], 0, 1).start()

            for k in range(1, kinds):
                cut(me, mids[1 - h], k, 0).start()

            @pl.when(odd)
            def _():
                for k in range(1, kinds):
                    cut(me, mids[1 - h], k, 1).start()

            across(1 - h).wait_recv()
            combine(full_ref, half_ref.at[0], half_ref.at[1])
            for s in others:
                handed(s).start()

            @pl.when(~odd)
            def _():
                for k in range(1, kinds):
                    cut(me, mids[1 - h], k, 1).start()

        for s in halves:
            @pl.when(me == s)
            def _():
                targets = (there if s not in mids else []) + [t for t in halves if t != s and t not in mids]
                for t in targets:
                    for k in range(kinds):
                        bulk(me, t, k).start()

    for g in range(groups):
        @pl.when(group != g)
        def _():
            swap(g, g).wait_recv()
    options = classes(users)
    choice = jnp.int32(0)
    for g in range(groups):
        pick = jnp.int32(0)
        for c, caps in enumerate(options):
            covers = None
            for u in range(users):
                source = mids[0] if u * quarter >= half else mids[1]
                most = source * per_dev + caps[u] * per_dev // 8
                fits = (blocks[g, u] * BLOCK <= most) if caps[u] < 8 else None
                if fits is not None:
                    covers = fits if covers is None else covers & fits
            pick = jnp.int32(c) if covers is None else jnp.where(covers, c, pick)
        choice = choice * len(options) + pick
    choice_ref[0] = choice

    @pl.when((me != ends[0]) & (me != ends[1]))
    def _():
        handed(me).wait_recv()

    for u in range(users):
        length = lengths_ref[u, :].astype(jnp.float32)
        for k in range(kinds):
            total, high, low = full_ref[0, k, u, :], full_ref[1, k, u, :], full_ref[2, k, u, :]
            center = total / length
            scale = jnp.maximum(high - center, center - low) + EPSILON
            centers_ref[k, u, :] = center
            scales_ref[k, u, :] = scale
            inverse_ref[k, u, :] = 1.0 / scale

    user = me // quarter
    base = (me % quarter) * part
    length = lengths_ref[pl.ds(user, 1), :]

    def normalise(source, k, rows):
        center = centers_ref[k, pl.ds(user, 1), :]
        inverse = inverse_ref[k, pl.ds(user, 1), :]
        step = part // 4

        def at(i):
            place = pl.ds(pl.multiple_of(source * part + i * step, step), step)
            first = source * per_dev + base + i * step
            recv_ref[k, place, :] = normalised(recv_ref[k, place, :], first, length, center, inverse)

        each(0, rows // step, at)

    own.wait()
    each(0, kinds, lambda k: normalise(me, k, part))

    def arrive(source):
        def at(k):
            bulk(source, me, k).wait_recv()
            normalise(source, k, part)

        each(0, kinds, at)

    for h in range(2):
        halves = range(h * half, (h + 1) * half)
        there = [s for s in range(n) if s // half != h and s not in mids]

        @pl.when(side == h)
        def _():
            @pl.when(outer)
            def _():
                for s in halves:
                    @pl.when(me != s)
                    def _():
                        arrive(s)

            for s in there:
                @pl.when(outer)
                def _():
                    arrive(s)

                @pl.when(mid)
                def _():
                    def at(k):
                        for i in range(2):
                            cut(s, me, k, i).wait_recv()
                        normalise(s, k, part)

                    each(0, kinds, at)

            for t in halves:
                if t not in mids:
                    @pl.when(me != t)
                    def _():
                        for k in range(kinds):
                            bulk(me, t, k).wait_send()

            @pl.when(outer)
            def _():
                for t in there:
                    for k in range(kinds):
                        bulk(me, t, k).wait_send()
                for k in range(kinds):
                    for i in range(2):
                        cut(me, mids[1 - h], k, i).wait_send()

            @pl.when(me != ends[h])
            def _():
                stat(me, ends[h]).wait_send()

            @pl.when(me == ends[h])
            def _():
                across(h).wait_send()
                for s in halves:
                    if s != ends[h]:
                        handed(s).wait_send()

    for g in range(groups):
        @pl.when(group != g)
        def _():
            swap(group, g).wait_send()


def remainder(index, n, groups, quarter, kv_ref, lengths_ref, centers_ref, inverse_ref, recv_ref,
              send_sem, recv_sem, near_send, near_recv, ready):
    kinds, users, per_dev, width = kv_ref.shape
    part = per_dev // quarter
    half = n // 2
    options = classes(users)
    me = lax.axis_index("seq")
    group = lax.axis_index("groups")
    mids = (half - 1, half)
    mid = (me == mids[0]) | (me == mids[1])
    outer = (me < mids[0]) | (me > mids[1])
    side = me // half

    barrier = pltpu.get_barrier_semaphore()
    for d in range(n):
        @pl.when(mid & (me != d))
        def _():
            pl.semaphore_signal(barrier, inc=1, device_id={"seq": d})

    @pl.when(mid)
    def _():
        pl.semaphore_wait(barrier, 1)

    @pl.when(outer)
    def _():
        pl.semaphore_wait(barrier, 2)
        for d in mids:
            pl.semaphore_signal(ready, inc=1, device_id={"seq": d})

    def window(target, caps):
        rows = caps[target // quarter] * per_dev // 8 - (target % quarter) * part
        return max(min(rows, part), 0)

    def late(target, caps, k):
        rows = window(target, caps)
        user, q = target // quarter, target % quarter
        return pltpu.make_async_remote_copy(
            src_ref=kv_ref.at[k, user, pl.ds(q * part, rows), :],
            dst_ref=recv_ref.at[k, pl.ds(0, rows), :],
            send_sem=send_sem.at[target, k],
            recv_sem=recv_sem.at[k],
            device_id={"seq": target},
        )

    def near(source, h, k):
        target = mids[h]
        user, q = target // quarter, target % quarter
        slot = 1 + (source if h == 0 else n - 1 - source)
        return pltpu.make_async_remote_copy(
            src_ref=kv_ref.at[k, user, pl.ds(q * part, part), :],
            dst_ref=recv_ref.at[k, pl.ds(slot * part, part), :],
            send_sem=near_send.at[k],
            recv_sem=near_recv.at[slot, k],
            device_id={"seq": target},
        )

    picks = []
    for g in reversed(range(groups)):
        picks.insert(0, options[index // len(options) ** (groups - 1 - g) % len(options)])

    def both(action):
        for g in range(groups):
            @pl.when(group == g)
            def _():
                action(picks[g])

    for h in range(2):
        for s in range(h * half, (h + 1) * half):
            if s not in mids:
                @pl.when(me == s)
                def _():
                    for k in range(kinds):
                        near(s, h, k).start()

    def split(h, caps):
        return kinds if 2 * window(mids[1 - h], caps) <= part else 1

    def send(targets, caps, which):
        for t in targets:
            for k in which:
                if window(t, caps):
                    late(t, caps, k).start()

    for h in range(2):
        away = [t for t in range(n) if t // half != h and t not in mids]

        @pl.when(me == mids[h])
        def _():
            both(lambda caps: send([mids[1 - h]], caps, range(split(h, caps))))
            if n > 2:
                pl.semaphore_wait(ready, n - 2)
            both(lambda caps: (
                send(away, caps, range(kinds)),
                send([mids[1 - h]], caps, range(split(h, caps), kinds)),
            ))

    user = me // quarter
    base = (me % quarter) * part
    length = lengths_ref[pl.ds(user, 1), :]
    step = part // 4

    def put(slot, source, k, i):
        center = centers_ref[k, pl.ds(user, 1), :]
        inverse = inverse_ref[k, pl.ds(user, 1), :]
        place = pl.ds(pl.multiple_of(slot * part + i * step, step), step)
        first = source * per_dev + base + i * step
        recv_ref[k, place, :] = normalised(recv_ref[k, place, :], first, length, center, inverse)

    def clear(k, i):
        recv_ref[k, pl.ds(pl.multiple_of(i * step, step), step), :] = jnp.zeros((step, width), jnp.bfloat16)

    for h in range(2):
        @pl.when(mid & (side == h))
        def _():
            for s in range(h * half, (h + 1) * half):
                if s not in mids:
                    slot = 1 + (s if h == 0 else n - 1 - s)
                    for k in range(kinds):
                        near(s, h, k).wait_recv()
                    each(0, kinds, lambda k: each(0, part // step, lambda i: put(slot, s, k, i)))

    def settle(t, caps):
        source = mids[1 - t // half]
        rows = window(t, caps)
        for k in range(kinds):
            each(rows // step, part // step, lambda i: clear(k, i))
        for k in range(kinds):
            if rows:
                late(t, caps, k).wait_recv()
                each(0, rows // step, lambda i: put(0, source, k, i))

    for t in range(n):
        @pl.when(me == t)
        def _():
            both(lambda caps: settle(t, caps))

    def drain(targets, caps):
        for t in targets:
            for k in range(kinds):
                if window(t, caps):
                    late(t, caps, k).wait_send()

    for h in range(2):
        away = [t for t in range(n) if t // half != h]

        @pl.when(me == mids[h])
        def _():
            both(lambda caps: drain(away, caps))

        for s in range(h * half, (h + 1) * half):
            if s not in mids:
                @pl.when(me == s)
                def _():
                    for k in range(kinds):
                        near(s, h, k).wait_send()


def finish(n, part, early_ref, late_ref, c_ref, s_ref, out_ref, centers_ref, scales_ref, sems):
    half = n // 2
    mids = (half - 1, half)
    me = lax.axis_index("seq")
    for t in range(n):
        @pl.when(me == t)
        def _():
            h = t // half
            pieces = []
            for s in range(n):
                at = s * part
                if s == mids[1 - h]:
                    pieces.append((late_ref, 0, at, part))
                elif t in mids and s != t and s // half == h:
                    pieces.append((late_ref, (1 + (s if h == 0 else n - 1 - s)) * part, at, part))
                elif pieces and pieces[-1][0] is early_ref:
                    _, a, b, rows = pieces.pop()
                    pieces.append((early_ref, a, b, rows + part))
                else:
                    pieces.append((early_ref, at, at, part))
            copies = [
                pltpu.make_async_copy(
                    ref.at[:, pl.ds(a, rows), :], out_ref.at[:, pl.ds(b, rows), :], sems.at[i])
                for i, (ref, a, b, rows) in enumerate(pieces)
            ] + [
                pltpu.make_async_copy(c_ref, centers_ref, sems.at[n]),
                pltpu.make_async_copy(s_ref, scales_ref, sems.at[n + 1]),
            ]
            for copy in copies:
                copy.start()
            for copy in copies:
                copy.wait()


def on_device(kv_cache, valid_blocks):
    kind_count, layer_dev, user_count, per_dev, heads_dev, width = kv_cache.shape
    n, groups = lax.axis_size("seq"), lax.axis_size("groups")
    quarter = n // user_count
    part = per_dev // quarter
    kinds = kind_count * layer_dev * heads_dev
    kv = jnp.transpose(kv_cache, (0, 1, 4, 2, 3, 5)).reshape(kinds, user_count, per_dev, width)
    kv = pltpu.with_memory_space_constraint(kv, pltpu.HBM)
    blocks = pltpu.with_memory_space_constraint(valid_blocks, pltpu.HBM)
    vmem = pl.BlockSpec(memory_space=pltpu.VMEM)
    smem = pl.BlockSpec(memory_space=pltpu.SMEM)
    anywhere = pl.BlockSpec(memory_space=pl.ANY)
    hbm = pl.BlockSpec(memory_space=pltpu.HBM)
    table = (3, kinds, user_count, width)
    dma = pltpu.SemaphoreType.DMA
    small = jax.ShapeDtypeStruct((kinds, user_count, width), jnp.float32)
    whole = jax.ShapeDtypeStruct((kinds, n * part, width), jnp.bfloat16)
    early, centers, scales, inverse, lengths, choice = pl.pallas_call(
        functools.partial(gather, n, groups, quarter),
        out_shape=(
            whole, small, small, small,
            jax.ShapeDtypeStruct((user_count, width), jnp.int32),
            jax.ShapeDtypeStruct((1,), jnp.int32),
        ),
        in_specs=[hbm, hbm],
        out_specs=(vmem,) * 5 + (smem,),
        scratch_shapes=[
            pltpu.SMEM((groups, user_count), jnp.int32),
            pltpu.VMEM((kinds, user_count, per_dev, width), jnp.bfloat16),
            pltpu.VMEM((n,) + table, jnp.float32),
            pltpu.VMEM((2,) + table, jnp.float32),
            pltpu.VMEM(table, jnp.float32),
            dma, dma, dma, dma((n, kinds)), dma((n, kinds)), dma((kinds, 2)), dma((n, kinds, 2)),
            dma, dma((n,)), dma, dma, dma((n,)), dma, dma((groups,)), dma((groups,)),
            pltpu.SemaphoreType.REGULAR,
        ],
        compiler_params=pltpu.CompilerParams(
            collective_id=0, has_side_effects=True, vmem_limit_bytes=GRANT
        ),
        name="gather",
    )(blocks, kv)

    def branch(index):
        def run(lengths, centers, inverse):
            return pl.pallas_call(
                functools.partial(remainder, index, n, groups, quarter),
                out_shape=jax.ShapeDtypeStruct((kinds, (n // 2) * part, width), jnp.bfloat16),
                in_specs=[hbm, vmem, vmem, vmem],
                out_specs=vmem,
                scratch_shapes=[
                    dma((n, kinds)), dma((kinds,)), dma((kinds,)), dma((n // 2, kinds)),
                    pltpu.SemaphoreType.REGULAR,
                ],
                compiler_params=pltpu.CompilerParams(
                    collective_id=1 + index, has_side_effects=True, vmem_limit_bytes=GRANT
                ),
                name=f"remainder_{index}",
            )(kv, lengths, centers, inverse)

        return run

    late = lax.switch(
        choice[0],
        [branch(i) for i in range(len(classes(user_count)) ** groups)],
        lengths, centers, inverse,
    )
    out, centers, scales = pl.pallas_call(
        functools.partial(finish, n, part),
        out_shape=(whole, small, small),
        in_specs=[vmem] * 4,
        out_specs=(anywhere, anywhere, anywhere),
        scratch_shapes=[dma((n + 2,))],
        compiler_params=pltpu.CompilerParams(vmem_limit_bytes=GRANT),
        name="finish",
    )(early, late, centers, scales)

    def spread(x, middle):
        x = x.reshape(kind_count, layer_dev, heads_dev, *middle, width)
        return jnp.moveaxis(x, 2, -2)

    return (
        spread(out, (1, n * part)),
        spread(centers, (user_count,)),
        spread(scales, (user_count,)),
    )


def solution(mesh):
    in_specs = (P(None, "layer", "groups", "seq", "head", None), P("groups"))
    out_specs = (
        P(None, "layer", ("groups", "seq"), None, "head", None),
        P(None, "layer", "groups", "head", None),
        P(None, "layer", "groups", "head", None),
    )
    return jax.shard_map(
        on_device, mesh=mesh, in_specs=in_specs, out_specs=out_specs, check_vma=False
    )
```

time: 50.6 us -> 53.2 us (1.051)
  Pallas kernels: 49.8 us -> 51.6 us
  between operations: 0.64 us -> 1.48 us
    pallas_call x2 -> x3, Pallas kernels: 49.8 us -> 51.6 us  [the longest x1 29.6 us: run(): pl.pallas_call(functools.partial(remainder, index, n, groups, quarter), o...]
where the time goes in v4:
time: 53.2 us; the launch traced here: 53.3 us
  Pallas kernels  51.6 us (97%)
  between operations  1.48 us (3%)
    pallas_call x1, Pallas kernels, run(): pl.pallas_call(functools.partial(remainder, index, n, groups, quarter), o...  29.6 us
    pallas_call x1, Pallas kernels, on_device(): pl.pallas_call(functools.partial(gather, n, groups, quarter), out_shape=(...  20.5 us
    pallas_call x1, Pallas kernels, on_device(): pl.pallas_call(functools.partial(finish, n, part), out_shape=(whole, smal...  1.39 us

profile of v4, /device:TPU:12, one launch (start us, length us, event | category | flops | bytes accessed | tf_op | source)
XLA Modules:
  0.0 53.3 jit_solution(11831207939553944949)
XLA Ops:
  0.6 20.5 %gather.1 = (bf16[2,4096,128]{2,1,0:T(8,128)(2,1)S(1)}, f32[2,4,128]{2,1,0:T(4,128)S(1)}, f32[2,4,128]{2,1,0:T(4,128)S(1)}, f32[2,4,128]{2,1,0:T(4,128)S(1)}, s32[4,128]{1,0:T(4,128)S(1)}, /*index=5*/s32[1]{0:T(128)}) custom-call(s32[4]{0:T(128)} %blocks_ref.1, bf16[2,4,1024,128]{3,2,1,0:T(8,128)(2,1)} %bitcast.11), custom_call_target="tpu_custom_call" | custom-call | tf_op jit(solution)/shard_map/gather/pallas_call | solution.py:592
  21.8 29.9 %conditional.1 = (bf16[2,2048,128]{2,1,0:T(8,128)(2,1)S(1)}) conditional(s32[]{:T(128)} %bitcast.1, (bf16[2,4,1024,128]{3,2,1,0:T(8,128)(2,1)}, s32[4,128]{1,0:T(4,128)S(1)}, f32[2,4,128]{2,1,0:T(4,128)S(1)}, f32[2,4,128]{2,1,0:T(4,128)S(1)}) %tuple.122, (bf16[2,4,1024,128]{3,2,1,0:T(8,128)(2,1)}, ...), branch_computations={%region_0.0_spmd, %region_1.0_spmd, %region_2.0_spmd, %region_3.0_... | conditional | bytes 8 | solution.py:636
  21.9 29.6 %remainder_0.1 = bf16[2,2048,128]{2,1,0:T(8,128)(2,1)S(1)} custom-call(bf16[2,4,1024,128]{3,2,1,0:T(8,128)(2,1)} %get-tuple-element.201.kv_ref, s32[4,128]{1,0:T(4,128)S(1)} %get-tuple-element.202.lengths_ref, f32[2,4,128]{2,1,0:T(4,128)S(1)} %get-tuple-element.203.centers_ref, f32[2,4,128]{2,1,0:T(4,128)S(1)} %get-tuple-element.204.inverse_ref), custom_call_target="tpu_custom_call" | custom-call | tf_op jit(solution)/shard_map/cond/branch_0_fun/remainder_0/pallas_call | solution.py:619
  51.7 1.4 %finish.1 = (bf16[2,4096,128]{2,1,0:T(8,128)(2,1)}, f32[2,4,128]{2,1,0:T(4,128)}, f32[2,4,128]{2,1,0:T(4,128)}) custom-call(bf16[2,4096,128]{2,1,0:T(8,128)(2,1)S(1)} %get-tuple-element.338.early_ref, bf16[2,2048,128]{2,1,0:T(8,128)(2,1)S(1)} %get-tuple-element.350.late_ref, f32[2,4,128]{2,1,0:T(4,128)S(1)} %get-tuple-element.341.c_ref, ...), custom_call_target="tpu_custom_call" | custom-call | tf_op jit(solution)/shard_map/finish/pallas_call | solution.py:641
